TPU v7x, 32 devices: a whole 2x2x4 slice. The times are simulated.
32 devices in a mesh: seq: 4 (over y, x), mem: 8 (over z, core).
Axes of the slice: x: 2, y: 2, z: 4, core: 2. Of those that a mesh axis runs over, the one named last changes fastest.
Arguments:
- hidden: bfloat16 [8192, 2048], P(('seq', 'mem')), may hold values from -6 to 6
- routes: int32 [8192, 2], P(('seq', 'mem')), may hold values from 0 to 7, all different within a row; in each aligned block of 256 rows (0 to 255, 256 to 511, ...) at most 64 rows name the same one
- gate_levels: int32 [8192, 2], P(('seq', 'mem')), may hold values from 1 to 255
- query_weight: bfloat16 [2048, 1024], P('seq'), may hold values from -0.125 to 0.125
- key_weight: bfloat16 [8, 2048, 1024], P('mem', 'seq'), may hold values from -0.125 to 0.125
- value_weight: bfloat16 [8, 2048, 1024], P('mem', 'seq'), may hold values from -0.125 to 0.125
Outputs:
- mixed: bfloat16 [8192, 1024], P(('seq', 'mem'))
Inputs may be any that keep to these rules, and one draw needn't show every extreme that they name: `routes`: the two memories of a row differ. In the rows of one device no memory is named by more than 64 rows, a bound that some block reaches.
All inputs are finite; a program needn't handle non-finite values.
Results may differ from a plain program's by a relative error of at most 0.01.
Values may be sent and summed in bfloat16 or wider, within the bound.
No kernel may reach another device: no remote copies, remote signals or barrier semaphores. Data moves between devices by JAX's collectives and lax.ppermute only.
A program may use at most 128 MiB of HBM per device.

v0:
```python
import jax
import jax.numpy as jnp
from jax import lax
from jax.sharding import PartitionSpec as P

HEADS = 8
DK = 128
BLOCK = 512
CAP = 64


def entering(array, axis, join, neutral):
    place = lax.axis_index(axis)
    gathered = lax.all_gather(array.astype(jnp.bfloat16), axis)
    state = jnp.zeros_like(array) + jnp.asarray(neutral, array.dtype)

    def one(step, state):
        return join(state, lax.dynamic_index_in_dim(gathered, step, 0, False).astype(array.dtype))

    return lax.fori_loop(0, place, one, state)


def add_states(earlier, later):
    return earlier + later


def on_device(hidden, routes, gate_levels, query_weight, key_weight, value_weight):
    count = hidden.shape[0]
    model = hidden.shape[1]
    width = query_weight.shape[1]
    mem_local = key_weight.shape[0]
    experts = mem_local * lax.axis_size("mem")
    highest = lax.Precision.HIGHEST
    onehot = (routes[:, :, None] == jnp.arange(experts, dtype=jnp.int32)[None, None, :]).astype(
        jnp.int32
    )
    per_token = jnp.sum(onehot, axis=1)
    before = jnp.cumsum(per_token, axis=0) - per_token
    place = jnp.sum(onehot * before[:, None, :], axis=2)
    slots = (routes * CAP + place).reshape(-1)
    owner_of = jnp.arange(2 * count, dtype=jnp.int32) // 2
    match = jnp.arange(experts * CAP, dtype=jnp.int32)[:, None] == slots[None, :]
    source = jnp.sum(jnp.where(match, owner_of[None, :], 0), axis=1)
    filled = jnp.any(match, axis=1)
    sent_rows = jnp.where(
        filled[:, None], jnp.take(hidden, source, axis=0), jnp.zeros((), hidden.dtype)
    )
    sent_rows = sent_rows.reshape(experts, CAP, model)
    columns = hidden
    queries = jnp.dot(
        columns,
        lax.all_gather(query_weight, "seq", axis=0, tiled=True),
        preferred_element_type=jnp.float32,
    ).astype(jnp.bfloat16)
    sent_queries = jnp.where(
        filled[:, None], jnp.take(queries, source, axis=0), jnp.zeros((), queries.dtype)
    )
    sent_queries = sent_queries.reshape(experts, CAP, width)
    arrived, arrived_queries = (
        lax.all_to_all(sent_rows, "mem", split_axis=0, concat_axis=1, tiled=True),
        lax.all_to_all(sent_queries, "mem", split_axis=0, concat_axis=1, tiled=True),
    )
    length = arrived.shape[1]
    columns = arrived
    key_part = jnp.einsum(
        "mrc,mch->mrh",
        columns,
        lax.all_gather(key_weight, "seq", axis=1, tiled=True),
        preferred_element_type=jnp.float32,
    )
    value_part = jnp.einsum(
        "mrc,mch->mrh",
        columns,
        lax.all_gather(value_weight, "seq", axis=1, tiled=True),
        preferred_element_type=jnp.float32,
    )
    keys = key_part
    values = value_part
    keys = keys.astype(jnp.bfloat16)
    values = values.astype(jnp.bfloat16)
    nblocks = length // BLOCK
    shape5 = (mem_local, nblocks, BLOCK, HEADS, DK)
    q_five = arrived_queries.reshape(shape5)
    k_five = keys.reshape(shape5)
    v_five = values.reshape(shape5)
    block_states = jnp.einsum(
        "mnkhd,mnkhe->mnhde", k_five, v_five, preferred_element_type=jnp.float32
    )
    within = jnp.cumsum(block_states, axis=1) - block_states
    local_total = jnp.sum(block_states, axis=1)
    nothing = jnp.zeros_like(local_total)
    incoming = entering(local_total, "seq", add_states, nothing)
    states = (incoming[:, None] + within).reshape(mem_local * nblocks, HEADS, DK, DK)
    flat = (mem_local * nblocks, BLOCK, HEADS, DK)
    rowids = jnp.arange(BLOCK, dtype=jnp.int32)
    causal = (rowids[:, None] >= rowids[None, :]).astype(jnp.float32)

    def attend(inputs):
        q_block, k_block, v_block, state = inputs
        scores = (
            jnp.einsum("qhd,khd->hqk", q_block, k_block, preferred_element_type=jnp.float32)
            * causal[None]
        )
        local = jnp.einsum("hqk,khd->qhd", scores, v_block.astype(jnp.float32), precision=highest)
        carried = jnp.einsum("qhd,hde->qhe", q_block.astype(jnp.float32), state, precision=highest)
        reads = local + carried
        scale = lax.rsqrt(jnp.mean(reads * reads, axis=-1, keepdims=True) + 1e-06)
        return (reads * scale).astype(jnp.bfloat16)

    normed = lax.map(
        attend, (q_five.reshape(flat), k_five.reshape(flat), v_five.reshape(flat), states)
    )
    normed = normed.reshape(mem_local, length, width)
    returned = lax.all_to_all(normed, "mem", split_axis=1, concat_axis=0, tiled=True)
    returned = returned.reshape(experts * CAP, width)
    picked = jnp.take(returned, slots, axis=0).reshape(count, 2, width)
    levels = gate_levels.astype(jnp.float32)
    gates = levels / jnp.sum(levels, axis=1, keepdims=True)
    mixed = jnp.sum(gates[:, :, None] * picked.astype(jnp.float32), axis=1)
    return mixed.astype(jnp.bfloat16)


def solution(mesh):
    return jax.shard_map(
        on_device,
        mesh=mesh,
        in_specs=(
            P(("seq", "mem"), None),
            P(("seq", "mem"), None),
            P(("seq", "mem"), None),
            P("seq", None),
            P("mem", "seq", None),
            P("mem", "seq", None),
        ),
        out_specs=P(("seq", "mem"), None),
        check_vma=False,
    )
```

profile of v0, /device:TPU:0, one launch (start us, length us, event | category | flops | bytes accessed | tf_op | source)
XLA Modules:
  0.0 289.7 jit_solution(13704537950358973058)
XLA Ops:
  10.6 2.5 gather_fusion
  13.5 55.2 %all_to_all.12 = bf16[8,64,2048]{2,1,0:T(8,128)(2,1)S(1)} all-to-all(bf16[8,64,2048]{2,1,0:T(8,128)(2,1)S(1)} %select_select_fusion), channel_id=1, replica_groups=mesh['seq'=4,'mem'=8] {'mem'}, dimensions={0} | all-to-all | bytes 4194304 | tf_op jit(solution)/shard_map/all_to_all | solution.py:60
  70.0 5.5 %fusion.15 = bf16[512,1024]{1,0:T(8,128)(2,1)} fusion(bf16[512,2048]{1,0:T(8,128)(2,1)S(1)} %bitcast.80, bf16[1,2048,1024]{2,1,0:T(8,128)(2,1)} %all-gather.10.cloned.1.call-done), kind=kOutput, calls=%fused_computation.20 | convolution fusion | flops 2148007936 | bytes 7340032 | tf_op jit(solution)/shard_map/mrc,mch->mrh/dot_general | solution.py:65
  75.5 1.6 copy.74
  77.1 41.9 %all-gather.6.cloned.1.call-done = bf16[1,2048,1024]{2,1,0:T(8,128)(2,1)} async-done(((bf16[1,512,1024]{2,1,0:T(8,128)(2,1)}), bf16[1,2048,1024]{2,1,0:T(8,128)(2,1)}) %all-gather.6.cloned.1.call-update) | async-done | bytes 4194320 | tf_op jit(solution)/shard_map/all_gather | solution.py:74
  119.0 5.2 %fusion.18 = bf16[64,8,8,128]{3,2,1,0:T(8,128)(2,1)S(1)} fusion(bf16[512,2048]{1,0:T(8,128)(2,1)} %bitcast.81, bf16[1,2048,1024]{2,1,0:T(8,128)(2,1)} %all-gather.6.cloned.1.call-done), kind=kOutput, calls=%fused_computation.21 | convolution fusion | flops 2148007936 | bytes 7340032 | tf_op jit(solution)/shard_map/mrc,mch->mrh/dot_general | solution.py:71
  126.3 47.1 %all-gather.8.cloned.1.call-done = bf16[2048,1024]{1,0:T(8,128)(2,1)} async-done(((bf16[512,1024]{1,0:T(8,128)(2,1)}), bf16[2048,1024]{1,0:T(8,128)(2,1)}) %all-gather.8.cloned.1.call-update) | async-done | bytes 4194320 | tf_op jit(solution)/shard_map/all_gather | solution.py:52
  173.5 3.4 %convolution_convert_fusion = bf16[256,1024]{1,0:T(8,128)(2,1)S(1)} fusion(bf16[256,2048]{1,0:T(8,128)(2,1)S(1)} %copy-done, bf16[2048,1024]{1,0:T(8,128)(2,1)} %all-gather.8.cloned.1.call-done), kind=kOutput, calls=%fused_computation.22 | convolution fusion | flops 1074003968 | bytes 5767168 | tf_op jit(solution)/shard_map/dot_general | solution.py:50
  176.9 2.8 gather_fusion.1
  179.7 2.4 select_select_fusion.1
  182.1 4.6 %all-to-all-start.1 = ((bf16[8,64,1024]{2,1,0:T(8,128)(2,1)}), bf16[8,64,1024]{2,1,0:T(8,128)(2,1)}, u32[]{:S(2)}, u32[]{:S(2)}) async-start(bf16[8,64,1024]{2,1,0:T(8,128)(2,1)} %select_select_fusion.1), calls=%async_computation.1 | async-start | bytes 2097152 | tf_op jit(solution)/shard_map/all_to_all | solution.py:61
  187.8 13.9 %all-gather.12.cloned.1.call-done = bf16[32,128,128]{2,1,0:T(8,128)(2,1)} async-done(((bf16[8,128,128]{2,1,0:T(8,128)(2,1)}), bf16[32,128,128]{2,1,0:T(8,128)(2,1)}) %all-gather.12.cloned.1.call-update) | async-done | bytes 1048592 | tf_op jit(solution)/shard_map/all_gather | solution.py:14
  201.9 11.5 %all-to-all-done.1 = bf16[8,64,1024]{2,1,0:T(8,128)(2,1)} async-done(((bf16[8,64,1024]{2,1,0:T(8,128)(2,1)}), bf16[8,64,1024]{2,1,0:T(8,128)(2,1)}, u32[]{:S(2)}, u32[]{:S(2)}) %all-to-all-start.1) | async-done | bytes 1048608 | tf_op jit(solution)/shard_map/all_to_all | solution.py:61
  213.4 1.5 copy.76
  217.7 5.5 %fusion.7 = (f32[512,8]{0,1:T(8,128)S(1)}, f32[8,128,512]{2,1,0:T(8,128)S(1)}) fusion(f32[8,128,512]{2,1,0:T(8,128)S(1)} %fusion.28, f32[8,512,512]{2,1,0:T(8,128)S(1)} %fusion.30, f32[512,512]{1,0:T(8,128)S(1)} %copy-done.1, bf16[64,8,8,128]{3,2,1,0:T(8,128)(2,1)S(1)} %copy-done.3), kind=kOutput, calls=%fused_computation.13 | convolution fusion | flops 3224891392 | bytes 14696448 | tf_op jit(solution)/shard_map/while/body/eval_jaxpr/hqk,khd->qhd/dot_general | solution.py:104
  224.5 4.7 %copy.70 = bf16[1,512,1024]{2,0,1:T(2,128)(2,1)S(1)} copy(bf16[1,512,1024]{1,2,0:T(8,128)(2,1)} %bitcast.78) | data formatting | bytes 2097152 | tf_op jit(solution)/shard_map/reshape | solution.py:113
  229.8 7.8 %reduce.2 = bf16[512,1024]{1,0:T(8,128)(2,1)} reduce(bf16[512,1,1024]{2,1,0:T(2,128)(2,1)S(1)} %bitcast.77, bf16[]{:T(256)} %broadcast.156), dimensions={1}, to_apply=%bitcast.55.reduce_sub_computation | reduce | bytes 2097154
  237.5 2.6 reshape.245
  240.2 3.6 %all-to-all-start.2 = ((bf16[8,2,32768]{2,1,0:T(2,128)(2,1)}), bf16[8,2,32768]{2,1,0:T(2,128)(2,1)S(1)}, u32[]{:S(2)}, u32[]{:S(2)}) async-start(bf16[8,2,32768]{2,1,0:T(2,128)(2,1)} %reshape.245), calls=%async_computation.2 | async-start | bytes 2097152 | tf_op jit(solution)/shard_map/all_to_all | solution.py:114
  244.3 26.0 %all-to-all-done.2 = bf16[8,2,32768]{2,1,0:T(2,128)(2,1)S(1)} async-done(((bf16[8,2,32768]{2,1,0:T(2,128)(2,1)}), bf16[8,2,32768]{2,1,0:T(2,128)(2,1)S(1)}, u32[]{:S(2)}, u32[]{:S(2)}) %all-to-all-start.2) | async-done | bytes 1048608 | tf_op jit(solution)/shard_map/all_to_all | solution.py:114
  270.2 3.5 %reshape.246 = bf16[512,1,1024]{2,1,0:T(2,128)(2,1)} reshape(bf16[8,2,32768]{2,1,0:T(2,128)(2,1)S(1)} %all-to-all-done.2) | data formatting | bytes 2097152
  273.7 2.0 copy.94
  275.6 2.1 gather_fusion.2
  278.2 5.0 %multiply_reduce_fusion = bf16[256,1024]{1,0:T(8,128)(2,1)} fusion(bf16[256,2,1024]{2,1,0:T(2,128)(2,1)S(1)} %gather.23, pred[256,2]{1,0:T(8,128)(4,1)S(1)} %copy.60, f32[256,2]{1,0:T(8,128)S(1)} %copy.59), kind=kLoop, calls=%fused_computation.15 | loop fusion | flops 1835008 | bytes 1575424 | tf_op jit(solution)/shard_map/reduce_sum | solution.py:119
  (59 shorter events, 14.7 us)
Async XLA Ops:
  6.5 4.1 %copy-start = (bf16[256,2048]{1,0:T(8,128)(2,1)S(1)}, bf16[256,2048]{1,0:T(8,128)(2,1)}, u32[]{:S(2)}) copy-start(bf16[256,2048]{1,0:T(8,128)(2,1)} %param.8) | copy-start | bytes 3145732
  6.5 2.3 copy-start.5
  6.5 62.1 %all-gather.10.cloned.1.call-start = ((), (), s32[]{:S(2)}) async-start(), calls=%async_computation.5 | async-start | bytes 5242880 | tf_op jit(solution)/shard_map/all_gather | solution.py:68
  7.3 111.8 %all-gather.6.cloned.1.call-start = ((), (), s32[]{:S(2)}) async-start(), calls=%async_computation.3 | async-start | bytes 5242880 | tf_op jit(solution)/shard_map/all_gather | solution.py:74
  8.0 165.5 %all-gather.8.cloned.1.call-start = ((), (), s32[]{:S(2)}) async-start(), calls=%async_computation.4 | async-start | bytes 5242880 | tf_op jit(solution)/shard_map/all_gather | solution.py:52
  8.7 193.0 %all-gather.12.cloned.1.call-start = ((), (), s32[]{:S(2)}) async-start(), calls=%async_computation.6 | async-start | bytes 1310720 | tf_op jit(solution)/shard_map/all_gather | solution.py:14
  68.7 1.4 copy-start.4
  124.2 1.0 copy-start.2
  182.1 31.3 %all-to-all-start.1 = ((bf16[8,64,1024]{2,1,0:T(8,128)(2,1)}), bf16[8,64,1024]{2,1,0:T(8,128)(2,1)}, u32[]{:S(2)}, u32[]{:S(2)}) async-start(bf16[8,64,1024]{2,1,0:T(8,128)(2,1)} %select_select_fusion.1), calls=%async_computation.1 | async-start | bytes 2097152 | tf_op jit(solution)/shard_map/all_to_all | solution.py:61
  216.1 1.2 copy-start.1
  216.2 1.5 copy-start.3
  237.5 6.5 %copy-start.6 = (s32[256,2]{0,1:T(2,128)S(1)}, s32[256,2]{0,1:T(2,128)}, u32[]{:S(2)}) copy-start(s32[256,2]{0,1:T(2,128)} %param.10) | copy-start | bytes 6148
  240.2 30.1 %all-to-all-start.2 = ((bf16[8,2,32768]{2,1,0:T(2,128)(2,1)}), bf16[8,2,32768]{2,1,0:T(2,128)(2,1)S(1)}, u32[]{:S(2)}, u32[]{:S(2)}) async-start(bf16[8,2,32768]{2,1,0:T(2,128)(2,1)} %reshape.245), calls=%async_computation.2 | async-start | bytes 2097152 | tf_op jit(solution)/shard_map/all_to_all | solution.py:114
Sparse Core Ops, SparseCore 0:
  9.2 55.3 all-gather.9
  66.4 52.5 all-gather.5
  120.9 52.5 all-gather.7
  175.2 26.4 all-gather.11
where the time goes:
time: 290 us
  waiting for transfers between devices  142 us (49%)
  blocking collectives  55.2 us (19%)
  local copies, waits for them, and re-layouts  28.1 us (10%)
  matrix products  23 us (8%)
  other arithmetic  19.1 us (7%)
  between operations  13.4 us (5%)
  starting transfers between devices  8.28 us (3%)
    all_to_all x1, blocking collectives, on_device(): lax.all_to_all(sent_rows, 'mem', split_axis=0, concat_axis=1, tiled=True)  55.2 us
    all_gather x1, waiting for transfers between devices, on_device(): lax.all_gather(query_weight, 'seq', axis=0, tiled=True)  47.1 us
    all_gather x1, waiting for transfers between devices, on_device(): lax.all_gather(value_weight, 'seq', axis=1, tiled=True)  41.9 us
    all_to_all x1, waiting for transfers between devices, on_device(): lax.all_to_all(normed, 'mem', split_axis=1, concat_axis=0, tiled=True)  26 us
    all_gather x1, waiting for transfers between devices, entering(): gathered = lax.all_gather(array.astype(jnp.bfloat16), axis)  13.9 us
    unnamed x19, local copies, waits for them, and re-layouts  12.9 us
    all_to_all x1, waiting for transfers between devices, on_device(): lax.all_to_all(sent_queries, 'mem', split_axis=0, concat_axis=1, tiled=True)  11.5 us
    unnamed x1, other arithmetic  7.77 us
  transfers between devices with their start and end apart: 6, of which 5 were waited for; matrix products, arithmetic and copies ran while one was open for 10% of the time, Pallas kernels for 0%

commit v1 on v0

--- a/solution.py
+++ b/solution.py
@@ -68,12 +68,37 @@
         lax.all_gather(key_weight, "seq", axis=1, tiled=True),
         preferred_element_type=jnp.float32,
     )
+    size, index, span = (lax.axis_size("seq"), lax.axis_index("seq"), value_weight.shape[1])
+    right = [(i, (i + 1) % size) for i in range(size)]
+    left = [(i, (i - 1) % size) for i in range(size)]
+    half = size // 2
+    from_left = from_right = value_weight
     value_part = jnp.einsum(
         "mrc,mch->mrh",
-        columns,
-        lax.all_gather(value_weight, "seq", axis=1, tiled=True),
+        lax.dynamic_slice_in_dim(columns, index * span, value_weight.shape[1], axis=2),
+        value_weight,
         preferred_element_type=jnp.float32,
     )
+    for k in range(1, half + 1):
+        from_left = lax.ppermute(from_left, "seq", right)
+        if k < size - half:
+            from_right = lax.ppermute(from_right, "seq", left)
+            value_part = value_part + jnp.einsum(
+                "mrc,mch->mrh",
+                lax.dynamic_slice_in_dim(
+                    columns, (index + k) % size * span, from_right.shape[1], axis=2
+                ),
+                from_right,
+                preferred_element_type=jnp.float32,
+            )
+        value_part = value_part + jnp.einsum(
+            "mrc,mch->mrh",
+            lax.dynamic_slice_in_dim(
+                columns, (index - k) % size * span, from_left.shape[1], axis=2
+            ),
+            from_left,
+            preferred_element_type=jnp.float32,
+        )
     keys = key_part
     values = value_part
     keys = keys.astype(jnp.bfloat16)

time: 290 us -> 279 us (0.962)
  blocking collectives: 55.2 us -> 0 us
  waiting for transfers between devices: 142 us -> 173 us
  starting transfers between devices: 8.28 us -> 17.6 us
  matrix products: 23 us -> 27.7 us
    ppermute x0 -> x3, waiting for transfers between devices: none -> 98.7 us  [the longest x2 71.5 us: on_device(): from_left = lax.ppermute(from_left, 'seq', right)]
    all_to_all x1 -> x0, blocking collectives: 55.2 us -> none  [on_device(): lax.all_to_all(sent_rows, 'mem', split_axis=0, concat_axis=1, tiled=True)]
    all_gather x1 -> x0, waiting for transfers between devices: 41.9 us -> none  [on_device(): lax.all_gather(value_weight, 'seq', axis=1, tiled=True)]
    all_gather x1, waiting for transfers between devices: 47.1 us -> 14.6 us  [on_device(): lax.all_gather(query_weight, 'seq', axis=0, tiled=True)]
    all_to_all x0 -> x1, waiting for transfers between devices: none -> 7.01 us  [on_device(): lax.all_to_all(sent_rows, 'mem', split_axis=0, concat_axis=1, tiled=True)]
    all_to_all x0 -> x1, starting transfers between devices: none -> 6.35 us  [on_device(): lax.all_to_all(sent_rows, 'mem', split_axis=0, concat_axis=1, tiled=True)]
    dot_general x1 -> x4, matrix products: 5.15 us -> 8.89 us  [the longest x2 4.25 us: on_device(): jnp.einsum('mrc,mch->mrh', lax.dynamic_slice_in_dim(columns, (index - k)...]
    ppermute x0 -> x3, starting transfers between devices: none -> 2.98 us  [the longest x2 1.55 us: on_device(): from_left = lax.ppermute(from_left, 'seq', right)]
  transfers between devices with their start and end apart: 6 -> 9, of which waited for: 5 -> 8; matrix products, arithmetic and copies ran while one was open for 10% -> 12% of each run, Pallas kernels for 0% -> 0%
where the time goes in v1:
time: 279 us; the launch traced here: 278 us
  waiting for transfers between devices  173 us (62%)
  matrix products  27.7 us (10%)
  local copies, waits for them, and re-layouts  25.5 us (9%)
  other arithmetic  20.5 us (7%)
  starting transfers between devices  17.6 us (6%)
  between operations  13.4 us (5%)
    ppermute x2, waiting for transfers between devices, on_device(): from_left = lax.ppermute(from_left, 'seq', right)  71.5 us
    ppermute x1, waiting for transfers between devices, on_device(): from_right = lax.ppermute(from_right, 'seq', left)  27.2 us
    all_to_all x1, waiting for transfers between devices, on_device(): lax.all_to_all(normed, 'mem', split_axis=1, concat_axis=0, tiled=True)  26 us
    all_gather x1, waiting for transfers between devices, on_device(): lax.all_gather(query_weight, 'seq', axis=0, tiled=True)  14.6 us
    all_gather x1, waiting for transfers between devices, entering(): gathered = lax.all_gather(array.astype(jnp.bfloat16), axis)  14 us
    all_to_all x1, waiting for transfers between devices, on_device(): lax.all_to_all(sent_queries, 'mem', split_axis=0, concat_axis=1, tiled=True)  11.3 us
    unnamed x21, local copies, waits for them, and re-layouts  10.3 us
    unnamed x1, other arithmetic  7.77 us
  transfers between devices with their start and end apart: 9, of which 8 were waited for; matrix products, arithmetic and copies ran while one was open for 12% of the time, Pallas kernels for 0%

profile of v1, /device:TPU:0, one launch (start us, length us, event | category | flops | bytes accessed | tf_op | source)
XLA Modules:
  0.0 277.8 jit_solution(18084477628756653757)
XLA Ops:
  9.9 2.5 gather_fusion
  14.1 6.4 %all-to-all-start = ((bf16[8,64,2048]{2,1,0:T(8,128)(2,1)}), bf16[8,64,2048]{2,1,0:T(8,128)(2,1)S(1)}, u32[]{:S(2)}, u32[]{:S(2)}) async-start(bf16[8,64,2048]{2,1,0:T(8,128)(2,1)} %select_select_fusion), calls=%async_computation | async-start | bytes 4194304 | tf_op jit(solution)/shard_map/all_to_all | solution.py:60
  23.4 39.0 %collective-permute-done.1 = bf16[1,512,1024]{2,1,0:T(8,128)(2,1)} collective-permute-done((bf16[1,512,1024]{2,1,0:T(8,128)(2,1)}, bf16[1,512,1024]{2,1,0:T(8,128)(2,1)}, u32[]{:S(2)}, u32[]{:S(2)}) %collective-permute-start.1) | collective-permute-done | bytes 1048608 | tf_op jit(solution)/shard_map/ppermute | solution.py:83
  62.4 7.0 %all-to-all-done = bf16[8,64,2048]{2,1,0:T(8,128)(2,1)S(1)} async-done(((bf16[8,64,2048]{2,1,0:T(8,128)(2,1)}), bf16[8,64,2048]{2,1,0:T(8,128)(2,1)S(1)}, u32[]{:S(2)}, u32[]{:S(2)}) %all-to-all-start) | async-done | bytes 2097184 | tf_op jit(solution)/shard_map/all_to_all | solution.py:60
  69.4 2.7 fusion.22
  74.1 27.2 %collective-permute-done = bf16[1,512,1024]{2,1,0:T(8,128)(2,1)} collective-permute-done((bf16[1,512,1024]{2,1,0:T(8,128)(2,1)}, bf16[1,512,1024]{2,1,0:T(8,128)(2,1)}, u32[]{:S(2)}, u32[]{:S(2)}) %collective-permute-start) | collective-permute-done | bytes 1048608 | tf_op jit(solution)/shard_map/ppermute | solution.py:85
  103.2 32.5 %collective-permute-done.2 = bf16[1,512,1024]{2,1,0:T(8,128)(2,1)} collective-permute-done((bf16[1,512,1024]{2,1,0:T(8,128)(2,1)}, bf16[1,512,1024]{2,1,0:T(8,128)(2,1)}, u32[]{:S(2)}, u32[]{:S(2)}) %collective-permute-start.2) | collective-permute-done | bytes 1048608 | tf_op jit(solution)/shard_map/ppermute | solution.py:83
  135.8 2.3 fusion.13
  138.1 6.1 %fusion.10 = bf16[512,1024]{1,0:T(8,128)(2,1)} fusion(bf16[512,2048]{1,0:T(8,128)(2,1)} %bitcast.98, bf16[1,2048,1024]{2,1,0:T(8,128)(2,1)} %all-gather.7.cloned.1.call-done), kind=kOutput, calls=%fused_computation.18 | convolution fusion | flops 2148007936 | bytes 7340032 | tf_op jit(solution)/shard_map/mrc,mch->mrh/dot_general | solution.py:65
  147.1 14.6 %all-gather.5.cloned.1.call-done = bf16[2048,1024]{1,0:T(8,128)(2,1)} async-done(((bf16[512,1024]{1,0:T(8,128)(2,1)}), bf16[2048,1024]{1,0:T(8,128)(2,1)}) %all-gather.5.cloned.1.call-update) | async-done | bytes 4194320 | tf_op jit(solution)/shard_map/all_gather | solution.py:52
  161.7 3.4 %convolution_convert_fusion = bf16[256,1024]{1,0:T(8,128)(2,1)S(1)} fusion(bf16[256,2048]{1,0:T(8,128)(2,1)S(1)} %copy-done, bf16[2048,1024]{1,0:T(8,128)(2,1)} %all-gather.5.cloned.1.call-done), kind=kOutput, calls=%fused_computation.20 | convolution fusion | flops 1074003968 | bytes 5767168 | tf_op jit(solution)/shard_map/dot_general | solution.py:50
  165.1 2.8 %gather_fusion.1 = bf16[512,1024]{1,0:T(8,128)(2,1)} fusion(bf16[256,1024]{1,0:T(8,128)(2,1)S(1)} %convolution_convert_fusion, s32[1024]{0:T(1024)S(1)} %pad_clamp_fusion.1), kind=kCustom, calls=%fused_computation.1 | custom fusion | bytes 2099200 | tf_op jit(solution)/shard_map/jit(_take)/gather | solution.py:56
  167.9 2.4 select_select_fusion.1
  170.4 4.6 %all-to-all-start.1 = ((bf16[8,64,1024]{2,1,0:T(8,128)(2,1)}), bf16[8,64,1024]{2,1,0:T(8,128)(2,1)}, u32[]{:S(2)}, u32[]{:S(2)}) async-start(bf16[8,64,1024]{2,1,0:T(8,128)(2,1)} %select_select_fusion.1), calls=%async_computation.1 | async-start | bytes 2097152 | tf_op jit(solution)/shard_map/all_to_all | solution.py:61
  176.1 14.0 %all-gather.9.cloned.1.call-done = bf16[32,128,128]{2,1,0:T(8,128)(2,1)} async-done(((bf16[8,128,128]{2,1,0:T(8,128)(2,1)}), bf16[32,128,128]{2,1,0:T(8,128)(2,1)}) %all-gather.9.cloned.1.call-update) | async-done | bytes 1048592 | tf_op jit(solution)/shard_map/all_gather | solution.py:14
  190.3 11.3 %all-to-all-done.1 = bf16[8,64,1024]{2,1,0:T(8,128)(2,1)} async-done(((bf16[8,64,1024]{2,1,0:T(8,128)(2,1)}), bf16[8,64,1024]{2,1,0:T(8,128)(2,1)}, u32[]{:S(2)}, u32[]{:S(2)}) %all-to-all-start.1) | async-done | bytes 1048608 | tf_op jit(solution)/shard_map/all_to_all | solution.py:61
  205.7 5.5 %fusion.5 = (f32[512,8]{0,1:T(8,128)S(1)}, f32[8,128,512]{2,1,0:T(8,128)S(1)}) fusion(f32[8,128,512]{2,1,0:T(8,128)S(1)} %fusion.28, f32[8,512,512]{2,1,0:T(8,128)S(1)} %fusion.30, f32[512,512]{1,0:T(8,128)S(1)} %copy-done.4, bf16[64,8,8,128]{3,2,1,0:T(8,128)(2,1)S(1)} %fusion.13), kind=kOutput, calls=%fused_computation.11 | convolution fusion | flops 3224891392 | bytes 14696448 | tf_op jit(solution)/shard_map/while/body/eval_jaxpr/hqk,khd->qhd/dot_general | solution.py:129
  212.6 4.7 %copy.70 = bf16[1,512,1024]{2,0,1:T(2,128)(2,1)S(1)} copy(bf16[1,512,1024]{1,2,0:T(8,128)(2,1)} %bitcast.100) | data formatting | bytes 2097152 | tf_op jit(solution)/shard_map/reshape | solution.py:138
  217.8 7.8 %reduce.2 = bf16[512,1024]{1,0:T(8,128)(2,1)} reduce(bf16[512,1,1024]{2,1,0:T(2,128)(2,1)S(1)} %bitcast.99, bf16[]{:T(256)} %broadcast.163), dimensions={1}, to_apply=%bitcast.73.reduce_sub_computation | reduce | bytes 2097154
  225.6 2.6 reshape.277
  228.2 3.6 %all-to-all-start.2 = ((bf16[8,2,32768]{2,1,0:T(2,128)(2,1)}), bf16[8,2,32768]{2,1,0:T(2,128)(2,1)S(1)}, u32[]{:S(2)}, u32[]{:S(2)}) async-start(bf16[8,2,32768]{2,1,0:T(2,128)(2,1)} %reshape.277), calls=%async_computation.2 | async-start | bytes 2097152 | tf_op jit(solution)/shard_map/all_to_all | solution.py:139
  232.3 26.0 %all-to-all-done.2 = bf16[8,2,32768]{2,1,0:T(2,128)(2,1)S(1)} async-done(((bf16[8,2,32768]{2,1,0:T(2,128)(2,1)}), bf16[8,2,32768]{2,1,0:T(2,128)(2,1)S(1)}, u32[]{:S(2)}, u32[]{:S(2)}) %all-to-all-start.2) | async-done | bytes 1048608 | tf_op jit(solution)/shard_map/all_to_all | solution.py:139
  258.3 3.5 %reshape.278 = bf16[512,1,1024]{2,1,0:T(2,128)(2,1)} reshape(bf16[8,2,32768]{2,1,0:T(2,128)(2,1)S(1)} %all-to-all-done.2) | data formatting | bytes 2097152
  266.2 5.0 %multiply_reduce_fusion = bf16[256,1024]{1,0:T(8,128)(2,1)} fusion(bf16[256,2,1024]{2,1,0:T(2,128)(2,1)S(1)} %gather.23, pred[256,2]{1,0:T(8,128)(4,1)S(1)} %copy.60, f32[256,2]{1,0:T(8,128)S(1)} %copy.59), kind=kLoop, calls=%fused_computation.13 | loop fusion | flops 1835008 | bytes 1575424 | tf_op jit(solution)/shard_map/reduce_sum | solution.py:144
  (68 shorter events, 26.9 us)
Async XLA Ops:
  6.5 3.3 %copy-start = (bf16[256,2048]{1,0:T(8,128)(2,1)S(1)}, bf16[256,2048]{1,0:T(8,128)(2,1)}, u32[]{:S(2)}) copy-start(bf16[256,2048]{1,0:T(8,128)(2,1)} %param.8) | copy-start | bytes 3145732
  6.5 1.5 copy-start.6
  6.5 131.5 %all-gather.7.cloned.1.call-start = ((), (), s32[]{:S(2)}) async-start(), calls=%async_computation.4 | async-start | bytes 5242880 | tf_op jit(solution)/shard_map/all_gather | solution.py:68
  7.3 154.4 %all-gather.5.cloned.1.call-start = ((), (), s32[]{:S(2)}) async-start(), calls=%async_computation.3 | async-start | bytes 5242880 | tf_op jit(solution)/shard_map/all_gather | solution.py:52
  14.1 55.4 %all-to-all-start = ((bf16[8,64,2048]{2,1,0:T(8,128)(2,1)}), bf16[8,64,2048]{2,1,0:T(8,128)(2,1)S(1)}, u32[]{:S(2)}, u32[]{:S(2)}) async-start(bf16[8,64,2048]{2,1,0:T(8,128)(2,1)} %select_select_fusion), calls=%async_computation | async-start | bytes 4194304 | tf_op jit(solution)/shard_map/all_to_all | solution.py:60
  20.4 169.7 %all-gather.9.cloned.1.call-start = ((), (), s32[]{:S(2)}) async-start(), calls=%async_computation.5 | async-start | bytes 1310720 | tf_op jit(solution)/shard_map/all_gather | solution.py:14
  20.5 42.0 %collective-permute-start.1 = (bf16[1,512,1024]{2,1,0:T(8,128)(2,1)}, bf16[1,512,1024]{2,1,0:T(8,128)(2,1)}, u32[]{:S(2)}, u32[]{:S(2)}) collective-permute-start(bf16[1,512,1024]{2,1,0:T(8,128)(2,1)} %param.13), channel_id=1, source_target_pairs={{0,8},{8,16},{16,24},{24,0},{1,9},{9,17},{17,25},{25,1},{2,10},{10... | collective-permute-start | bytes 3145736 | tf_op jit(solution)/shard_map/ppermute | solution.py:83
  22.0 79.3 %collective-permute-start = (bf16[1,512,1024]{2,1,0:T(8,128)(2,1)}, bf16[1,512,1024]{2,1,0:T(8,128)(2,1)}, u32[]{:S(2)}, u32[]{:S(2)}) collective-permute-start(bf16[1,512,1024]{2,1,0:T(8,128)(2,1)} %param.13), channel_id=1, source_target_pairs={{0,24},{8,0},{16,8},{24,16},{1,25},{9,1},{17,9},{25,17},{2,26},{10... | collective-permute-start | bytes 3145736 | tf_op jit(solution)/shard_map/ppermute | solution.py:85
  62.4 73.3 %collective-permute-start.2 = (bf16[1,512,1024]{2,1,0:T(8,128)(2,1)}, bf16[1,512,1024]{2,1,0:T(8,128)(2,1)}, u32[]{:S(2)}, u32[]{:S(2)}) collective-permute-start(bf16[1,512,1024]{2,1,0:T(8,128)(2,1)} %collective-permute-done.1), channel_id=1, source_target_pairs={{0,8},{8,16},{16,24},{24,0},{1,9},{9,17},{17,25},{25,1},{2,10},{10... | collective-permute-start | bytes 3145736 | tf_op jit(solution)/shard_map/ppermute | solution.py:83
  69.4 31.8 %copy-start.3 = (bf16[8,64,2048]{2,1,0:T(8,128)(2,1)}, bf16[8,64,2048]{2,1,0:T(8,128)(2,1)S(1)}, u32[]{:S(2)}) copy-start(bf16[8,64,2048]{2,1,0:T(8,128)(2,1)S(1)} %all-to-all-done) | copy-start | bytes 6291460
  145.7 1.4 copy-start.1
  170.4 31.3 %all-to-all-start.1 = ((bf16[8,64,1024]{2,1,0:T(8,128)(2,1)}), bf16[8,64,1024]{2,1,0:T(8,128)(2,1)}, u32[]{:S(2)}, u32[]{:S(2)}) async-start(bf16[8,64,1024]{2,1,0:T(8,128)(2,1)} %select_select_fusion.1), calls=%async_computation.1 | async-start | bytes 2097152 | tf_op jit(solution)/shard_map/all_to_all | solution.py:61
  201.6 1.6 copy-start.2
  203.2 1.3 copy-start.5
  204.5 1.2 copy-start.4
  225.6 6.5 %copy-start.7 = (s32[256,2]{0,1:T(2,128)S(1)}, s32[256,2]{0,1:T(2,128)}, u32[]{:S(2)}) copy-start(s32[256,2]{0,1:T(2,128)} %param.10) | copy-start | bytes 6148
  228.2 30.1 %all-to-all-start.2 = ((bf16[8,2,32768]{2,1,0:T(2,128)(2,1)}), bf16[8,2,32768]{2,1,0:T(2,128)(2,1)S(1)}, u32[]{:S(2)}, u32[]{:S(2)}) async-start(bf16[8,2,32768]{2,1,0:T(2,128)(2,1)} %reshape.277), calls=%async_computation.2 | async-start | bytes 2097152 | tf_op jit(solution)/shard_map/all_to_all | solution.py:139
Sparse Core Ops, SparseCore 0:
  9.2 87.1 all-gather.6
  98.3 63.3 all-gather.4
  163.5 26.4 all-gather.8
